TPU v7x, 512 devices: a 8x2x16 block of a 8x8x16 slice. The times are simulated.
512 devices in a mesh: grp: 2 (over y), seq: 16 (over z), head: 8 (over x), rep: 2 (over core).
Axes of the slice: x: 8, y: 2, z: 16, core: 2. Of those that a mesh axis runs over, the one named last changes fastest.
The devices are a block of a 8x8x16 slice.
Arguments:
- queries: bfloat16 [16, 4096], P(('grp', 'rep'), 'head'), parts along dimension 0, may hold values from -6 to 6
- k_cache: bfloat16 [16, 16, 16384, 128], P(('grp', 'rep'), 'head', 'seq'), parts along dimension 0, may hold values from -6 to 6
- v_cache: bfloat16 [16, 16, 16384, 128], P(('grp', 'rep'), 'head', 'seq'), parts along dimension 0, may hold values from -6 to 6
- page_table: int32 [16, 128], P(('grp', 'rep')), parts along dimension 0, may hold values from 0 to 127, each once within a row
- lengths: int32 [16], P(('grp', 'rep')), parts along dimension 0, may hold values from 2048 to 16384
- keep_threshold: int32 [16, 16], P(('grp', 'rep'), 'head'), parts along dimension 0, may hold values from 256 to 8191
Outputs:
- attended: bfloat16 [16, 4096], P(('grp', 'rep'), 'head'), parts along dimension 0
- token_mass: float32 [16, 16, 16384], P(('grp', 'rep'), 'head', 'seq'), parts along dimension 0
- page_keep: float32 [16, 16, 128], P(('grp', 'rep'), 'head', 'seq'), parts along dimension 0
There are 2 independent parts, one for each index of `grp`. A program takes and returns all parts, laid end to end along the dimension named above; each array names one. Nothing has to cross between parts.
Inputs may be any that keep to these rules, and one draw needn't show every extreme that they name: `page_table`: each row names every physical page slot 0 to 127 once.
All inputs are finite; a program needn't handle non-finite values.
Results may differ from a plain program's by a relative error of at most 0.0052.
Values sent between devices are 32-bit elements; how exact they have to be, the bound alone decides.
A program may use at most 64 MiB of HBM per device.

v0:
```python
import jax
import jax.numpy as jnp
from jax import lax
from jax.sharding import PartitionSpec as P

PAGE = 128


softcap = 50.0
query_scale = 1.0 / 12.0
quanta = 65536.0


def sent_to_all(shard, axis):
    size = lax.axis_size(axis)
    return lax.all_to_all(
        jnp.broadcast_to(shard[None], (size, *shard.shape)), axis, 0, 0, tiled=True
    )


def of_everyone(shard, axis):
    everything = sent_to_all(shard, axis)
    return jnp.sum(everything, axis=0)


def packed_total(arrays, axis):
    ravelled, at, outs = (jnp.concatenate([a.reshape(-1) for a in arrays]), 0, [])
    total = of_everyone(ravelled, axis)
    for a in arrays:
        outs.append(total[at : at + a.size].reshape(a.shape))
        at += a.size
    return tuple(outs)


def shards(queries, k_cache, v_cache, page_table, lengths, keep_threshold):
    requests, kv_local, tok_local, head_size = k_cache.shape
    q_local = queries.shape[1] // head_size
    group = q_local // kv_local
    pages_local = tok_local // PAGE
    pages_all = page_table.shape[1]
    seq_index = lax.axis_index("seq")
    slot_ids = seq_index * pages_local + jnp.arange(pages_local, dtype=jnp.int32)
    matches = page_table[:, None, :] == slot_ids[None, :, None]
    logical = jnp.sum(
        jnp.where(matches, jnp.arange(pages_all, dtype=jnp.int32)[None, None, :], 0), axis=2
    )
    position = (
        logical[:, :, None] * PAGE + jnp.arange(PAGE, dtype=jnp.int32)[None, None, :]
    ).reshape(requests, tok_local)
    is_live = position < lengths[:, None]
    grouped = queries.reshape(requests, kv_local, group, head_size)
    logits = jnp.einsum("rkgd,rktd->rkgt", grouped, k_cache, preferred_element_type=jnp.float32)
    capped = softcap * jnp.tanh(logits * query_scale / softcap)
    weights = jnp.where(is_live[:, None, None, :], jnp.exp(capped - softcap), 0.0)
    denom_part = jnp.sum(weights, axis=3)
    numer_part = jnp.einsum(
        "rkgt,rktd->rkgd", weights.astype(jnp.bfloat16), v_cache, preferred_element_type=jnp.float32
    )
    denom, numer = packed_total((denom_part, numer_part), "seq")
    attended = (
        (numer / denom[..., None]).astype(jnp.bfloat16).reshape(requests, q_local * head_size)
    )
    payload = jnp.sum(weights / denom[..., None], axis=2).reshape(
        requests, kv_local, pages_local, PAGE
    )
    mine = seq_index * pages_local + jnp.arange(pages_local, dtype=jnp.int32)
    my_pages = jnp.sum(
        jnp.where(
            jnp.arange(pages_all, dtype=jnp.int32)[None, None, :] == mine[None, :, None],
            page_table[:, None, :],
            0,
        ),
        axis=2,
    )
    piece = lax.all_gather(payload, "seq", axis=2, tiled=True)
    count = piece.shape[2]
    phys = jnp.arange(count, dtype=jnp.int32)
    select = (my_pages[:, None, :] == phys[None, :, None]).astype(jnp.float32)
    owned = jnp.einsum("rxic,rim->rxmc", piece, select, precision=lax.Precision.HIGHEST)
    owned = owned.reshape(requests, payload.shape[1], tok_local)
    page_mass = jnp.sum(owned.reshape(requests, kv_local, pages_local, PAGE), axis=3)
    page_keep = jnp.minimum(
        1.0, quanta * page_mass / keep_threshold.astype(jnp.float32)[:, :, None]
    )
    return (attended, owned, page_keep)


def solution(mesh):
    placed = (
        P(("grp", "rep"), "head"),
        P(("grp", "rep"), "head", "seq", None),
        P(("grp", "rep"), "head", "seq", None),
        P(("grp", "rep"), None),
        P(("grp", "rep")),
        P(("grp", "rep"), "head"),
    )
    return jax.shard_map(
        shards,
        mesh=mesh,
        in_specs=placed,
        out_specs=(
            P(("grp", "rep"), "head"),
            P(("grp", "rep"), "head", "seq"),
            P(("grp", "rep"), "head", "seq"),
        ),
        check_vma=False,
    )
```

profile of v0, /device:TPU:78, one launch (start us, length us, event | category | flops | bytes accessed | tf_op | source)
XLA Modules:
  0.0 99.6 jit_solution(83259887863694445)
XLA Ops:
  0.6 0.0 copy-start
  0.7 0.1 iota_compare_fusion.1
  0.7 1.0 %select_reduce_fusion = (s32[4,8]{1,0:T(4,128)S(1)}, s32[4,8]{1,0:T(4,128)S(1)}) fusion(s32[4,128]{1,0:T(4,128)} %param.9, pred[8,128]{1,0:T(8,128)(4,1)S(1)} %iota_compare_fusion.1, s32[8]{0:T(128)S(1)} %iota_add_fusion), kind=kLoop, calls=%fused_computation.13 | loop fusion | flops 20416 | bytes 3360 | tf_op jit(solution)/shard_map/reduce_sum | solution.py:67
  1.8 0.1 broadcast_bitcast_fusion
  1.9 0.7 reshape.98
  2.6 0.7 fusion.7
  3.3 0.0 copy-done
  3.3 0.0 copy-start.1
  3.3 0.8 fusion.11
  4.1 0.1 reshape.99
  4.2 2.0 %fusion.5 = f32[4,2,2,128]{3,2,1,0:T(2,128)S(1)} fusion(bf16[4,2,1024,128]{3,2,1,0:T(8,128)(2,1)} %param.8, f32[4,2,2,1024]{3,2,1,0:T(2,128)S(1)} %get-tuple-element.6), kind=kOutput, calls=%fused_computation.8 | convolution fusion | flops 4210688 | bytes 2170880 | tf_op jit(solution)/shard_map/rkgt,rktd->rkgd/dot_general | solution.py:56
  6.1 0.1 pad_maximum_fusion
  6.2 0.7 broadcast_in_dim.72
  6.9 43.7 %all-to-all-start = ((f32[16,1,2064]{2,1,0:T(1,128)}), f32[16,1,2064]{2,1,0:T(1,128)S(1)}, u32[]{:S(2)}, u32[]{:S(2)}) async-start(f32[16,1,2064]{2,1,0:T(1,128)} %broadcast_in_dim.72), calls=%async_computation | async-start | bytes 278528 | tf_op jit(solution)/shard_map/all_to_all | solution.py:16
  50.6 0.0 copy-done.1
  50.7 0.1 copy.13
  50.8 14.6 %all-to-all-done = f32[16,1,2064]{2,1,0:T(1,128)S(1)} async-done(((f32[16,1,2064]{2,1,0:T(1,128)}), f32[16,1,2064]{2,1,0:T(1,128)S(1)}, u32[]{:S(2)}, u32[]{:S(2)}) %all-to-all-start) | async-done | bytes 132128 | tf_op jit(solution)/shard_map/all_to_all | solution.py:16
  65.3 0.1 reduce_sum.56
  65.4 0.1 slice.16
  65.5 0.1 div.36
  65.6 0.2 divide_reduce_fusion
  65.8 0.1 div.37
  65.9 31.4 %all_gather.3 = f32[4,2,128,128]{3,2,1,0:T(8,128)S(1)} all-gather(f32[4,2,8,128]{3,2,1,0:T(8,128)S(1)} %reshape.102), channel_id=1, replica_groups=mesh['grp'=2,'seq'=16,'head'=8,'rep'=2] {'seq'}, dimensions={2}, use_global_device_ids=true | all-gather | bytes 557056 | tf_op jit(solution)/shard_map/all_gather | solution.py:75
  97.3 0.4 fusion.12
  97.6 0.6 reshape.103
  98.3 0.6 divide_convert_fusion
  98.9 0.7 divide_minimum_fusion
  (8 shorter events, 0.1 us)
Async XLA Ops:
  0.6 2.7 %copy-start = (bf16[4,2,1024,128]{3,2,1,0:T(8,128)(2,1)S(1)}, bf16[4,2,1024,128]{3,2,1,0:T(8,128)(2,1)}, u32[]{:S(2)}) copy-start(bf16[4,2,1024,128]{3,2,1,0:T(8,128)(2,1)} %param.7) | copy-start | bytes 6291460
  3.3 47.3 %copy-start.1 = (s32[4,2]{0,1:T(2,128)S(1)}, s32[4,2]{0,1:T(2,128)}, u32[]{:S(2)}) copy-start(s32[4,2]{0,1:T(2,128)} %param.11) | copy-start | bytes 100
  6.9 58.4 %all-to-all-start = ((f32[16,1,2064]{2,1,0:T(1,128)}), f32[16,1,2064]{2,1,0:T(1,128)S(1)}, u32[]{:S(2)}, u32[]{:S(2)}) async-start(f32[16,1,2064]{2,1,0:T(1,128)} %broadcast_in_dim.72), calls=%async_computation | async-start | bytes 278528 | tf_op jit(solution)/shard_map/all_to_all | solution.py:16
where the time goes:
time: 99.8 us; the launch traced here: 99.6 us
  starting transfers between devices  43.7 us (44%)
  blocking collectives  31.4 us (31%)
  waiting for transfers between devices  14.6 us (15%)
  other arithmetic  3.47 us (3%)
  matrix products  3.11 us (3%)
  local copies, waits for them, and re-layouts  2.63 us (3%)
    all_to_all x1, starting transfers between devices, sent_to_all(): lax.all_to_all(jnp.broadcast_to(shard[None], (size, *shard.shape)), axis,...  43.7 us
    all_gather x1, blocking collectives, shards(): piece = lax.all_gather(payload, 'seq', axis=2, tiled=True)  31.4 us
    all_to_all x1, waiting for transfers between devices, sent_to_all(): lax.all_to_all(jnp.broadcast_to(shard[None], (size, *shard.shape)), axis,...  14.6 us
  transfers between devices with their start and end apart: 1, of which 1 were waited for; matrix products, arithmetic and copies ran while one was open for 0% of the time, Pallas kernels for 0%

commit v1 on v0

v1 whole, which is shorter than its diff:
```python
import jax
import jax.numpy as jnp
from jax import lax
from jax.experimental import pallas as pl
from jax.experimental.pallas import tpu as pltpu
from jax.sharding import PartitionSpec as P

PAGE = 128
SUBS = 4
MESH = pl.DeviceIdType.MESH

softcap = 50.0
query_scale = 1.0 / 12.0
quanta = 65536.0


def attend(
    q_ref, pt_vec, pt_ref, len_ref, thr_ref, k_hbm, v_hbm,
    att_ref, mass_ref, keep_ref,
    kbuf, vbuf, gath, part, att32, k_sem, v_sem, g_send, g_recv, p_send, p_recv,
):
    n = lax.axis_size("seq")
    z = lax.axis_index("seq")
    requests = k_hbm.shape[0]
    pairs = requests // 2
    slots = k_hbm.shape[2] // PAGE
    per = slots // SUBS

    def ring(step):
        return lax.rem(z + step + 2 * n, n)

    copies = []
    for r in range(requests):
        k_copy = pltpu.make_async_copy(k_hbm.at[r], kbuf.at[r], k_sem.at[r])
        k_copy.start()
        copies.append(k_copy)
    v_copies = []
    for r in range(requests):
        v_copy = pltpu.make_async_copy(v_hbm.at[r], vbuf.at[r], v_sem.at[r])
        v_copy.start()
        v_copies.append(v_copy)
    barrier = pltpu.get_barrier_semaphore()
    for step in (1, -1):
        pl.semaphore_signal(barrier, inc=1, device_id={"seq": ring(step)}, device_id_type=MESH)

    sub = lax.broadcasted_iota(jnp.int32, (8, PAGE), 0)
    lane = lax.broadcasted_iota(jnp.int32, (8, PAGE), 1)
    first = lax.rem(sub, 4) < 2
    queries = q_ref[...].astype(jnp.float32)

    def rows_of(even, odd):
        return jnp.where(first, even, odd)

    weights = []
    denoms = []
    for p in range(pairs):
        logits = None
        for ri in range(2):
            r = 2 * p + ri
            lhs = []
            for kv in range(2):
                row = ri * 2 + kv
                block = jnp.where(
                    sub == row,
                    queries[r : r + 1, (2 * kv) * PAGE : (2 * kv + 1) * PAGE],
                    jnp.where(
                        sub == 4 + row,
                        queries[r : r + 1, (2 * kv + 1) * PAGE : (2 * kv + 2) * PAGE],
                        0.0,
                    ),
                )
                lhs.append(block)
            lhs = jnp.concatenate(lhs, axis=1).astype(jnp.bfloat16)
            copies[r].wait()
            keys = jnp.concatenate([kbuf[r, 0], kbuf[r, 1]], axis=1)
            term = lax.dot_general(
                lhs, keys, (((1,), (1,)), ((), ())), preferred_element_type=jnp.float32
            )
            logits = term if logits is None else logits + term
        table = rows_of(pt_vec[2 * p : 2 * p + 1, :], pt_vec[2 * p + 1 : 2 * p + 2, :])
        length = rows_of(len_ref[2 * p], len_ref[2 * p + 1])
        total = None
        tiles = []
        for s in range(slots):
            hit = jnp.where(table == z * slots + s, lane, 0).astype(jnp.float32)
            logical = jnp.sum(hit, axis=1, keepdims=True).astype(jnp.int32)
            live = logical * PAGE + lane < length
            tile = logits[:, s * PAGE : (s + 1) * PAGE]
            capped = softcap * jnp.tanh(tile * query_scale / softcap)
            tile = jnp.where(live, jnp.exp(capped - softcap), 0.0)
            gath[z * slots + s, p] = tile
            tiles.append(tile)
            total = tile if total is None else total + tile
        weights.append(jnp.concatenate(tiles, axis=1).astype(jnp.bfloat16))
        denoms.append(jnp.sum(total, axis=1, keepdims=True))
    part[z, 2] = jnp.where(lane == 0, denoms[0], denoms[1])

    pl.semaphore_wait(barrier, 2)

    def chunk_copy(src, way, step, c):
        block = gath.at[pl.ds(src * slots + c * per, per)]
        return pltpu.make_async_remote_copy(
            src_ref=block, dst_ref=block,
            send_sem=g_send.at[way, step, c], recv_sem=g_recv.at[way, step, c],
            device_id={"seq": ring(1 - 2 * way)}, device_id_type=MESH,
        )

    def part_copy(src, way, step):
        return pltpu.make_async_remote_copy(
            src_ref=part.at[src], dst_ref=part.at[src],
            send_sem=p_send.at[way, step], recv_sem=p_recv.at[way, step],
            device_id={"seq": ring(1 - 2 * way)}, device_id_type=MESH,
        )

    half = n // 2
    def goes(way, step, c):
        if step < half - 1:
            return True
        return c % 2 == way

    def part_goes(way, step):
        return step < half - 1 or way == 0

    sent = []

    def start(copy):
        copy.start()
        sent.append(copy)

    for c in range(SUBS):
        for way in range(2):
            if goes(way, 0, c):
                start(chunk_copy(z, way, 0, c))

    for p in range(pairs):
        numer = jnp.zeros((8, PAGE), jnp.float32)
        for ri in range(2):
            r = 2 * p + ri
            v_copies[r].wait()
            values = jnp.concatenate([vbuf[r, 0], vbuf[r, 1]], axis=1)
            out = jnp.dot(weights[p], values, preferred_element_type=jnp.float32)
            for kv in range(2):
                mine = lax.rem(sub, 4) == ri * 2 + kv
                numer = jnp.where(mine, out[:, kv * PAGE : (kv + 1) * PAGE], numer)
        part[z, p] = numer
    for way in range(2):
        start(part_copy(z, way, 0))

    for step in range(half):
        for c in range(SUBS):
            for way in range(2):
                if not goes(way, step, c):
                    continue
                src = ring((2 * way - 1) * (step + 1))
                chunk_copy(src, way, step, c).wait_recv()
                if step + 1 < half and goes(way, step + 1, c):
                    start(chunk_copy(src, way, step + 1, c))
        for way in range(2):
            if not part_goes(way, step):
                continue
            src = ring((2 * way - 1) * (step + 1))
            part_copy(src, way, step).wait_recv()
            if step + 1 < half and part_goes(way, step + 1):
                start(part_copy(src, way, step + 1))

    den = jnp.sum(part[:, 2], axis=0)
    for p in range(pairs):
        inv = 1.0 / jnp.sum(jnp.where(lane == p, den, 0.0), axis=1, keepdims=True)
        numer = jnp.sum(part[:, p], axis=0) * inv
        for ri in range(2):
            r = 2 * p + ri
            for kv in range(2):
                for g in range(2):
                    row = g * 4 + ri * 2 + kv
                    h = 2 * kv + g
                    att32[r : r + 1, h * PAGE : (h + 1) * PAGE] = numer[row : row + 1]
        keep = jnp.zeros((4, slots), jnp.float32)
        for j in range(slots):
            even = gath[pt_ref[2 * p, z * slots + j], p]
            odd = gath[pt_ref[2 * p + 1, z * slots + j], p]
            tile = rows_of(even, odd) * inv
            mass = tile[:4] + tile[4:]
            for ri in range(2):
                mass_ref[2 * p + ri, :, j * PAGE : (j + 1) * PAGE] = mass[2 * ri : 2 * ri + 2]
            page = jnp.sum(mass, axis=1, keepdims=True)
            column = lax.broadcasted_iota(jnp.int32, (4, slots), 1)
            keep = jnp.where(column == j, page, keep)
        for ri in range(2):
            r = 2 * p + ri
            which = lax.broadcasted_iota(jnp.int32, (2, slots), 0)
            thr = jnp.where(which == 0, thr_ref[0, r], thr_ref[1, r]).astype(jnp.float32)
            keep_ref[r] = jnp.minimum(1.0, quanta * keep[2 * ri : 2 * ri + 2] / thr)
    att_ref[...] = att32[...].astype(att_ref.dtype)
    for copy in sent:
        copy.wait_send()


def shards(queries, k_cache, v_cache, page_table, lengths, keep_threshold):
    n = lax.axis_size("seq")
    requests, kv_local, tok_local, head_size = k_cache.shape
    slots = tok_local // PAGE
    vmem = pl.BlockSpec(memory_space=pltpu.VMEM)
    smem = pl.BlockSpec(memory_space=pltpu.SMEM)
    hbm = pl.BlockSpec(memory_space=pl.ANY)
    dma = pltpu.SemaphoreType.DMA
    half = n // 2
    return pl.pallas_call(
        attend,
        out_shape=(
            jax.ShapeDtypeStruct(queries.shape, jnp.bfloat16),
            jax.ShapeDtypeStruct((requests, kv_local, tok_local), jnp.float32),
            jax.ShapeDtypeStruct((requests, kv_local, slots), jnp.float32),
        ),
        in_specs=[vmem, vmem, smem, smem, smem, hbm, hbm],
        out_specs=(vmem, vmem, vmem),
        scratch_shapes=[
            pltpu.VMEM(k_cache.shape, k_cache.dtype),
            pltpu.VMEM(v_cache.shape, v_cache.dtype),
            pltpu.VMEM((n * slots, requests // 2, 8, PAGE), jnp.float32),
            pltpu.VMEM((n, 3, 8, PAGE), jnp.float32),
            pltpu.VMEM(queries.shape, jnp.float32),
            dma((requests,)), dma((requests,)),
            dma((2, half, SUBS)), dma((2, half, SUBS)),
            dma((2, half)), dma((2, half)),
        ],
        compiler_params=pltpu.CompilerParams(collective_id=0, has_side_effects=True),
    )(queries, page_table, page_table, lengths, keep_threshold.T, k_cache, v_cache)


def solution(mesh):
    placed = (
        P(("grp", "rep"), "head"),
        P(("grp", "rep"), "head", "seq", None),
        P(("grp", "rep"), "head", "seq", None),
        P(("grp", "rep"), None),
        P(("grp", "rep")),
        P(("grp", "rep"), "head"),
    )
    return jax.shard_map(
        shards,
        mesh=mesh,
        in_specs=placed,
        out_specs=(
            P(("grp", "rep"), "head"),
            P(("grp", "rep"), "head", "seq"),
            P(("grp", "rep"), "head", "seq"),
        ),
        check_vma=False,
    )
```

time: 99.8 us -> 78 us (0.78)
  Pallas kernels: 0 us -> 73.1 us
  starting transfers between devices: 43.7 us -> 0 us
  blocking collectives: 31.4 us -> 0 us
  waiting for transfers between devices: 14.6 us -> 0 us
  other arithmetic: 3.47 us -> 0 us
  matrix products: 3.11 us -> 0 us
  local copies, waits for them, and re-layouts: 2.63 us -> 3.92 us
    pallas_call x0 -> x1, Pallas kernels: none -> 73.1 us  [shards(): pl.pallas_call(attend, out_shape=(jax.ShapeDtypeStruct(queries.shape, jnp...]
    all_to_all x1 -> x0, starting transfers between devices: 43.7 us -> none  [sent_to_all(): lax.all_to_all(jnp.broadcast_to(shard[None], (size, *shard.shape)), axis,...]
    all_gather x1 -> x0, blocking collectives: 31.4 us -> none  [shards(): piece = lax.all_gather(payload, 'seq', axis=2, tiled=True)]
    all_to_all x1 -> x0, waiting for transfers between devices: 14.6 us -> none  [sent_to_all(): lax.all_to_all(jnp.broadcast_to(shard[None], (size, *shard.shape)), axis,...]
    unnamed x5 -> x3, local copies, waits for them, and re-layouts: 0.09 us -> 3.92 us
    dot_general x3 -> x0, matrix products: 3.11 us -> none  [the longest x1 1.98 us: shards(): jnp.einsum('rkgt,rktd->rkgd', weights.astype(jnp.bfloat16), v_cache, pref...]
    reshape x5 -> x0, local copies, waits for them, and re-layouts: 1.46 us -> none  [the longest x1 0.7 us: shards(): grouped = queries.reshape(requests, kv_local, group, head_size)]
    reduce_sum x3 -> x0, other arithmetic: 1.31 us -> none  [the longest x1 1.04 us: shards(): jnp.sum(jnp.where(jnp.arange(pages_all, dtype=jnp.int32)[None, None, :] =...]
  transfers between devices with their start and end apart: 1 -> 0, of which waited for: 1 -> 0; matrix products, arithmetic and copies ran while one was open for 0% -> 0% of each run, Pallas kernels for 0% -> 0%
where the time goes in v1:
time: 78 us; the launch traced here: 77.7 us
  Pallas kernels  73.1 us (94%)
  local copies, waits for them, and re-layouts  3.92 us (5%)
    pallas_call x1, Pallas kernels, shards(): pl.pallas_call(attend, out_shape=(jax.ShapeDtypeStruct(queries.shape, jnp...  73.1 us
    unnamed x3, local copies, waits for them, and re-layouts  3.92 us

profile of v1, /device:TPU:78, one launch (start us, length us, event | category | flops | bytes accessed | tf_op | source)
XLA Modules:
  0.0 77.7 jit_solution(3313250800694432622)
XLA Ops:
  0.6 73.1 %shard_map.85 = (bf16[4,512]{1,0:T(4,128)(2,1)}, f32[4,2,1024]{2,1,0:T(2,128)}, f32[4,2,8]{2,1,0:T(2,128)}) custom-call(bf16[4,512]{1,0:T(4,128)(2,1)} %q_ref.1, s32[4,128]{1,0:T(4,128)} %pt_ref.1, s32[4,128]{1,0:T(4,128)} %pt_ref.1, s32[4]{0:T(128)} %len_ref.1, s32[2,4]{1,0:T(2,128)} %bitcast.1, bf16[4,2,1024,128]{3,2,1,0:T(8,128)(2,1)} %k_hbm.1, ...), custom_call_target="tpu_custom_call" | custom-call | tf_op jit(solution)/shard_map/pallas_call | solution.py:207
  73.8 1.3 %copy.12 = bf16[4,512]{1,0:T(4,128)(2,1)} copy(bf16[4,512]{1,0:T(4,128)(2,1)} %get-tuple-element.6) | data formatting | bytes 8192
  75.0 1.4 %copy.13 = f32[4,2,1024]{2,1,0:T(2,128)} copy(f32[4,2,1024]{2,1,0:T(2,128)} %get-tuple-element.7) | data formatting | bytes 65536
  76.4 1.3 %copy.14 = f32[4,2,8]{2,1,0:T(2,128)} copy(f32[4,2,8]{2,1,0:T(2,128)} %get-tuple-element.8) | data formatting | bytes 512

commit v2 on v1

--- a/solution.py
+++ b/solution.py
@@ -6,7 +6,7 @@
 from jax.sharding import PartitionSpec as P
 
 PAGE = 128
-SUBS = 4
+CUTS = 2
 MESH = pl.DeviceIdType.MESH
 
 softcap = 50.0
@@ -17,17 +17,17 @@
 def attend(
     q_ref, pt_vec, pt_ref, len_ref, thr_ref, k_hbm, v_hbm,
     att_ref, mass_ref, keep_ref,
-    kbuf, vbuf, gath, part, att32, k_sem, v_sem, g_send, g_recv, p_send, p_recv,
+    kbuf, vbuf, gath, part, att32, k_sem, v_sem,
+    g_recv, p_recv, own_send, own_part_send, fwd_send, fwd_part_send, ready,
 ):
     n = lax.axis_size("seq")
     z = lax.axis_index("seq")
     requests = k_hbm.shape[0]
     pairs = requests // 2
     slots = k_hbm.shape[2] // PAGE
-    per = slots // SUBS
-
-    def ring(step):
-        return lax.rem(z + step + 2 * n, n)
+    per = slots // CUTS
+    inner = z < n - 1
+    after = z > 0
 
     copies = []
     for r in range(requests):
@@ -39,9 +39,20 @@
         v_copy = pltpu.make_async_copy(v_hbm.at[r], vbuf.at[r], v_sem.at[r])
         v_copy.start()
         v_copies.append(v_copy)
+
     barrier = pltpu.get_barrier_semaphore()
-    for step in (1, -1):
-        pl.semaphore_signal(barrier, inc=1, device_id={"seq": ring(step)}, device_id_type=MESH)
+
+    @pl.when(after)
+    def _():
+        pl.semaphore_wait(barrier, 1)
+
+    @pl.when(inner)
+    def _():
+        pl.semaphore_signal(barrier, inc=1, device_id={"seq": z + 1}, device_id_type=MESH)
+
+    @pl.when(after)
+    def _():
+        pl.semaphore_signal(ready, inc=1, device_id={"seq": z - 1}, device_id_type=MESH)
 
     sub = lax.broadcasted_iota(jnp.int32, (8, PAGE), 0)
     lane = lax.broadcasted_iota(jnp.int32, (8, PAGE), 1)
@@ -50,6 +61,21 @@
 
     def rows_of(even, odd):
         return jnp.where(first, even, odd)
+
+    def chunk_copy(src, p, c, send_sem, target):
+        block = gath.at[p, pl.ds(src * slots + c * per, per)]
+        return pltpu.make_async_remote_copy(
+            src_ref=block, dst_ref=block,
+            send_sem=send_sem, recv_sem=g_recv.at[src, p, c],
+            device_id={"seq": target}, device_id_type=MESH,
+        )
+
+    def part_copy(src, send_sem, target):
+        return pltpu.make_async_remote_copy(
+            src_ref=part.at[src], dst_ref=part.at[src],
+            send_sem=send_sem, recv_sem=p_recv.at[src],
+            device_id={"seq": target}, device_id_type=MESH,
+        )
 
     weights = []
     denoms = []
@@ -88,50 +114,18 @@
             tile = logits[:, s * PAGE : (s + 1) * PAGE]
             capped = softcap * jnp.tanh(tile * query_scale / softcap)
             tile = jnp.where(live, jnp.exp(capped - softcap), 0.0)
-            gath[z * slots + s, p] = tile
+            gath[p, z * slots + s] = tile
             tiles.append(tile)
             total = tile if total is None else total + tile
         weights.append(jnp.concatenate(tiles, axis=1).astype(jnp.bfloat16))
         denoms.append(jnp.sum(total, axis=1, keepdims=True))
+
+        @pl.when(after)
+        def _():
+            for c in range(CUTS):
+                chunk_copy(z, p, c, own_send.at[p, c], 0).start()
+
     part[z, 2] = jnp.where(lane == 0, denoms[0], denoms[1])
-
-    pl.semaphore_wait(barrier, 2)
-
-    def chunk_copy(src, way, step, c):
-        block = gath.at[pl.ds(src * slots + c * per, per)]
-        return pltpu.make_async_remote_copy(
-            src_ref=block, dst_ref=block,
-            send_sem=g_send.at[way, step, c], recv_sem=g_recv.at[way, step, c],
-            device_id={"seq": ring(1 - 2 * way)}, device_id_type=MESH,
-        )
-
-    def part_copy(src, way, step):
-        return pltpu.make_async_remote_copy(
-            src_ref=part.at[src], dst_ref=part.at[src],
-            send_sem=p_send.at[way, step], recv_sem=p_recv.at[way, step],
-            device_id={"seq": ring(1 - 2 * way)}, device_id_type=MESH,
-        )
-
-    half = n // 2
-    def goes(way, step, c):
-        if step < half - 1:
-            return True
-        return c % 2 == way
-
-    def part_goes(way, step):
-        return step < half - 1 or way == 0
-
-    sent = []
-
-    def start(copy):
-        copy.start()
-        sent.append(copy)
-
-    for c in range(SUBS):
-        for way in range(2):
-            if goes(way, 0, c):
-                start(chunk_copy(z, way, 0, c))
-
     for p in range(pairs):
         numer = jnp.zeros((8, PAGE), jnp.float32)
         for ri in range(2):
@@ -143,25 +137,40 @@
                 mine = lax.rem(sub, 4) == ri * 2 + kv
                 numer = jnp.where(mine, out[:, kv * PAGE : (kv + 1) * PAGE], numer)
         part[z, p] = numer
-    for way in range(2):
-        start(part_copy(z, way, 0))
-
-    for step in range(half):
-        for c in range(SUBS):
-            for way in range(2):
-                if not goes(way, step, c):
-                    continue
-                src = ring((2 * way - 1) * (step + 1))
-                chunk_copy(src, way, step, c).wait_recv()
-                if step + 1 < half and goes(way, step + 1, c):
-                    start(chunk_copy(src, way, step + 1, c))
-        for way in range(2):
-            if not part_goes(way, step):
-                continue
-            src = ring((2 * way - 1) * (step + 1))
-            part_copy(src, way, step).wait_recv()
-            if step + 1 < half and part_goes(way, step + 1):
-                start(part_copy(src, way, step + 1))
+
+    @pl.when(after)
+    def _():
+        part_copy(z, own_part_send, 0).start()
+
+    @pl.when(inner)
+    def _():
+        pl.semaphore_wait(ready, 1)
+
+    def relay(src, carry):
+        other = src != z
+        passes = jnp.logical_and(inner, src != z + 1)
+        for p in range(pairs):
+            for c in range(CUTS):
+
+                @pl.when(other)
+                def _():
+                    chunk_copy(src, p, c, fwd_send.at[src, p, c], 0).wait_recv()
+
+                @pl.when(passes)
+                def _():
+                    chunk_copy(src, p, c, fwd_send.at[src, p, c], z + 1).start()
+
+        @pl.when(other)
+        def _():
+            part_copy(src, fwd_part_send.at[src], 0).wait_recv()
+
+        @pl.when(passes)
+        def _():
+            part_copy(src, fwd_part_send.at[src], z + 1).start()
+
+        return carry
+
+    lax.fori_loop(0, n, relay, 0)
 
     den = jnp.sum(part[:, 2], axis=0)
     for p in range(pairs):
@@ -176,8 +185,8 @@
                     att32[r : r + 1, h * PAGE : (h + 1) * PAGE] = numer[row : row + 1]
         keep = jnp.zeros((4, slots), jnp.float32)
         for j in range(slots):
-            even = gath[pt_ref[2 * p, z * slots + j], p]
-            odd = gath[pt_ref[2 * p + 1, z * slots + j], p]
+            even = gath[p, pt_ref[2 * p, z * slots + j]]
+            odd = gath[p, pt_ref[2 * p + 1, z * slots + j]]
             tile = rows_of(even, odd) * inv
             mass = tile[:4] + tile[4:]
             for ri in range(2):
@@ -191,8 +200,36 @@
             thr = jnp.where(which == 0, thr_ref[0, r], thr_ref[1, r]).astype(jnp.float32)
             keep_ref[r] = jnp.minimum(1.0, quanta * keep[2 * ri : 2 * ri + 2] / thr)
     att_ref[...] = att32[...].astype(att_ref.dtype)
-    for copy in sent:
-        copy.wait_send()
+
+    @pl.when(after)
+    def _():
+        for p in range(pairs):
+            for c in range(CUTS):
+                chunk_copy(z, p, c, own_send.at[p, c], 0).wait_send()
+        part_copy(z, own_part_send, 0).wait_send()
+
+    def drain(src, carry):
+        @pl.when(jnp.logical_and(inner, src != z + 1))
+        def _():
+            for p in range(pairs):
+                for c in range(CUTS):
+                    chunk_copy(src, p, c, fwd_send.at[src, p, c], 0).wait_send()
+            part_copy(src, fwd_part_send.at[src], 0).wait_send()
+
+        return carry
+
+    lax.fori_loop(0, n, drain, 0)
+
+
+def put_out(*refs):
+    count = len(refs) // 2
+    sems = refs[-1]
+    ins, outs = refs[:count], refs[count : 2 * count]
+    moves = [pltpu.make_async_copy(i, o, sems.at[k]) for k, (i, o) in enumerate(zip(ins, outs))]
+    for move in moves:
+        move.start()
+    for move in moves:
+        move.wait()
 
 
 def shards(queries, k_cache, v_cache, page_table, lengths, keep_threshold):
@@ -203,28 +240,38 @@
     smem = pl.BlockSpec(memory_space=pltpu.SMEM)
     hbm = pl.BlockSpec(memory_space=pl.ANY)
     dma = pltpu.SemaphoreType.DMA
-    half = n // 2
-    return pl.pallas_call(
+    pairs = requests // 2
+    results = (
+        (queries.shape, jnp.bfloat16),
+        ((requests, kv_local, tok_local), jnp.float32),
+        ((requests, kv_local, slots), jnp.float32),
+    )
+    held = pl.pallas_call(
         attend,
-        out_shape=(
-            jax.ShapeDtypeStruct(queries.shape, jnp.bfloat16),
-            jax.ShapeDtypeStruct((requests, kv_local, tok_local), jnp.float32),
-            jax.ShapeDtypeStruct((requests, kv_local, slots), jnp.float32),
-        ),
+        out_shape=tuple(pltpu.VMEM(*result) for result in results),
         in_specs=[vmem, vmem, smem, smem, smem, hbm, hbm],
         out_specs=(vmem, vmem, vmem),
         scratch_shapes=[
             pltpu.VMEM(k_cache.shape, k_cache.dtype),
             pltpu.VMEM(v_cache.shape, v_cache.dtype),
-            pltpu.VMEM((n * slots, requests // 2, 8, PAGE), jnp.float32),
+            pltpu.VMEM((pairs, n * slots, 8, PAGE), jnp.float32),
             pltpu.VMEM((n, 3, 8, PAGE), jnp.float32),
             pltpu.VMEM(queries.shape, jnp.float32),
             dma((requests,)), dma((requests,)),
-            dma((2, half, SUBS)), dma((2, half, SUBS)),
-            dma((2, half)), dma((2, half)),
+            dma((n, pairs, CUTS)), dma((n,)),
+            dma((pairs, CUTS)), dma,
+            dma((n, pairs, CUTS)), dma((n,)),
+            pltpu.SemaphoreType.REGULAR,
         ],
         compiler_params=pltpu.CompilerParams(collective_id=0, has_side_effects=True),
     )(queries, page_table, page_table, lengths, keep_threshold.T, k_cache, v_cache)
+    return pl.pallas_call(
+        put_out,
+        out_shape=tuple(jax.ShapeDtypeStruct(*result) for result in results),
+        in_specs=[vmem] * 3,
+        out_specs=(hbm, hbm, hbm),
+        scratch_shapes=[dma((3,))],
+    )(*(pltpu.with_memory_space_constraint(h, pltpu.VMEM) for h in held))
 
 
 def solution(mesh):

time: 78 us -> 71.5 us (0.917)
  the two profiles are of different devices: /device:TPU:78 before, /device:TPU:1728 now
where the time goes in v2:
time: 71.5 us; the launch traced here: 71.3 us
  Pallas kernels  70.7 us (99%)
    pallas_call x1, Pallas kernels, shards(): pl.pallas_call(attend, out_shape=tuple((pltpu.VMEM(*result) for result in...  70 us

profile of v2, /device:TPU:1728, one launch (start us, length us, event | category | flops | bytes accessed | tf_op | source)
XLA Modules:
  0.0 71.3 jit_solution(12851963935269687876)
XLA Ops:
  0.6 70.0 %shard_map.85 = (bf16[4,512]{1,0:T(4,128)(2,1)S(1)}, f32[4,2,1024]{2,1,0:T(2,128)S(1)}, f32[4,2,8]{2,1,0:T(2,128)S(1)}) custom-call(bf16[4,512]{1,0:T(4,128)(2,1)} %q_ref.1, s32[4,128]{1,0:T(4,128)} %pt_ref.1, s32[4,128]{1,0:T(4,128)} %pt_ref.1, s32[4]{0:T(128)} %len_ref.1, s32[2,4]{1,0:T(2,128)} %bitcast.1, bf16[4,2,1024,128]{3,2,1,0:T(8,128)(2,1)} %k_hbm.1, ...), custom_call_target="tpu_custom_call" | custom-call | tf_op jit(solution)/shard_map/pallas_call | solution.py:249
  70.7 0.6 shard_map.86

commit v3 on v2

--- a/solution.py
+++ b/solution.py
@@ -7,6 +7,7 @@
 
 PAGE = 128
 CUTS = 2
+TAIL = 2
 MESH = pl.DeviceIdType.MESH
 
 softcap = 50.0
@@ -18,7 +19,8 @@
     q_ref, pt_vec, pt_ref, len_ref, thr_ref, k_hbm, v_hbm,
     att_ref, mass_ref, keep_ref,
     kbuf, vbuf, gath, part, att32, k_sem, v_sem,
-    g_recv, p_recv, own_send, own_part_send, fwd_send, fwd_part_send, ready,
+    g_recv, p_recv, own_send, own_part_send, fwd_send, fwd_part_send, zero_send, zero_part_send,
+    ready, zero_ready,
 ):
     n = lax.axis_size("seq")
     z = lax.axis_index("seq")
@@ -26,8 +28,10 @@
     pairs = requests // 2
     slots = k_hbm.shape[2] // PAGE
     per = slots // CUTS
-    inner = z < n - 1
-    after = z > 0
+    edge = z == 0
+    hub = z == 1
+    follows = z > 1
+    passes_on = jnp.logical_and(z > 0, z < n - 1)
 
     copies = []
     for r in range(requests):
@@ -42,17 +46,23 @@
 
     barrier = pltpu.get_barrier_semaphore()
 
-    @pl.when(after)
-    def _():
-        pl.semaphore_wait(barrier, 1)
-
-    @pl.when(inner)
-    def _():
-        pl.semaphore_signal(barrier, inc=1, device_id={"seq": z + 1}, device_id_type=MESH)
-
-    @pl.when(after)
-    def _():
-        pl.semaphore_signal(ready, inc=1, device_id={"seq": z - 1}, device_id_type=MESH)
+    def greet(target):
+        pl.semaphore_signal(barrier, inc=1, device_id={"seq": target}, device_id_type=MESH)
+
+    @pl.when(hub)
+    def _():
+        greet(0)
+        for other in range(2, n - TAIL):
+            greet(other)
+
+    @pl.when(edge)
+    def _():
+        for other in range(n - TAIL, n):
+            greet(other)
+
+    @pl.when(passes_on)
+    def _():
+        greet(z + 1)
 
     sub = lax.broadcasted_iota(jnp.int32, (8, PAGE), 0)
     lane = lax.broadcasted_iota(jnp.int32, (8, PAGE), 1)
@@ -76,6 +86,20 @@
             send_sem=send_sem, recv_sem=p_recv.at[src],
             device_id={"seq": target}, device_id_type=MESH,
         )
+
+    direct = jnp.logical_or(edge, follows)
+    target = jnp.where(jnp.logical_or(edge, z < n - TAIL), 1, 0)
+
+    def greeted():
+        @pl.when(edge)
+        def _():
+            pl.semaphore_wait(barrier, 1)
+            pl.semaphore_signal(zero_ready, inc=1, device_id={"seq": 1}, device_id_type=MESH)
+
+        @pl.when(follows)
+        def _():
+            pl.semaphore_wait(barrier, 2)
+            pl.semaphore_signal(ready, inc=1, device_id={"seq": z - 1}, device_id_type=MESH)
 
     weights = []
     denoms = []
@@ -120,10 +144,13 @@
         weights.append(jnp.concatenate(tiles, axis=1).astype(jnp.bfloat16))
         denoms.append(jnp.sum(total, axis=1, keepdims=True))
 
-        @pl.when(after)
-        def _():
-            for c in range(CUTS):
-                chunk_copy(z, p, c, own_send.at[p, c], 0).start()
+        if p == 0:
+            greeted()
+
+        @pl.when(direct)
+        def _():
+            for c in range(CUTS):
+                chunk_copy(z, p, c, own_send.at[p, c], target).start()
 
     part[z, 2] = jnp.where(lane == 0, denoms[0], denoms[1])
     for p in range(pairs):
@@ -138,39 +165,87 @@
                 numer = jnp.where(mine, out[:, kv * PAGE : (kv + 1) * PAGE], numer)
         part[z, p] = numer
 
-    @pl.when(after)
-    def _():
-        part_copy(z, own_part_send, 0).start()
-
-    @pl.when(inner)
-    def _():
-        pl.semaphore_wait(ready, 1)
-
-    def relay(src, carry):
-        other = src != z
-        passes = jnp.logical_and(inner, src != z + 1)
+    @pl.when(direct)
+    def _():
+        part_copy(z, own_part_send, target).start()
+
+    def arrive(src):
         for p in range(pairs):
             for c in range(CUTS):
-
-                @pl.when(other)
+                chunk_copy(src, p, c, fwd_send.at[src, p, c], 0).wait_recv()
+        part_copy(src, fwd_part_send.at[src], 0).wait_recv()
+
+    def relay(src, goes_to, arrives, sends, chunk_sems, part_sems):
+        for p in range(pairs):
+            for c in range(CUTS):
+
+                @pl.when(arrives)
                 def _():
                     chunk_copy(src, p, c, fwd_send.at[src, p, c], 0).wait_recv()
 
-                @pl.when(passes)
+                @pl.when(sends)
                 def _():
-                    chunk_copy(src, p, c, fwd_send.at[src, p, c], z + 1).start()
-
-        @pl.when(other)
+                    chunk_copy(src, p, c, chunk_sems.at[src, p, c], goes_to).start()
+
+        @pl.when(arrives)
         def _():
             part_copy(src, fwd_part_send.at[src], 0).wait_recv()
 
-        @pl.when(passes)
-        def _():
-            part_copy(src, fwd_part_send.at[src], z + 1).start()
-
+        @pl.when(sends)
+        def _():
+            part_copy(src, part_sems.at[src], goes_to).start()
+
+    half = n // 2
+    yes = z >= 0
+    no = z < 0
+
+    def down(src, carry):
+        sends = jnp.logical_and(z < n - 1, src != z + 1)
+        relay(src, z + 1, src != z, sends, fwd_send, fwd_part_send)
         return carry
 
-    lax.fori_loop(0, n, relay, 0)
+    def up(src, carry):
+        relay(src, 0, no, yes, zero_send, zero_part_send)
+        return carry
+
+    def both(src, carry):
+        down(src, carry)
+
+        @pl.when(hub)
+        def _():
+            up(src, carry)
+
+        return carry
+
+    @pl.when(passes_on)
+    def _():
+        pl.semaphore_wait(ready, 1)
+
+    @pl.when(jnp.logical_not(edge))
+    def _():
+        lax.fori_loop(1, half, down, 0)
+
+        @pl.when(hub)
+        def _():
+            pl.semaphore_wait(zero_ready, 1)
+            lax.fori_loop(1, half, up, 0)
+
+        lax.fori_loop(half, n - TAIL, both, 0)
+        down(0, 0)
+        lax.fori_loop(n - TAIL, n, down, 0)
+
+    @pl.when(edge)
+    def _():
+        def hand_on(src, carry):
+            relay(src, 1, yes, yes, fwd_send, fwd_part_send)
+            return carry
+
+        def take(src, carry):
+            arrive(src)
+            return carry
+
+        lax.fori_loop(n - TAIL, n, hand_on, 0)
+        lax.fori_loop(1, n - TAIL, take, 0)
 
     den = jnp.sum(part[:, 2], axis=0)
     for p in range(pairs):
@@ -201,20 +276,29 @@
             keep_ref[r] = jnp.minimum(1.0, quanta * keep[2 * ri : 2 * ri + 2] / thr)
     att_ref[...] = att32[...].astype(att_ref.dtype)
 
-    @pl.when(after)
+    @pl.when(direct)
     def _():
         for p in range(pairs):
             for c in range(CUTS):
                 chunk_copy(z, p, c, own_send.at[p, c], 0).wait_send()
         part_copy(z, own_part_send, 0).wait_send()
 
+    def left(src, chunk_sems, part_sems):
+        for p in range(pairs):
+            for c in range(CUTS):
+                chunk_copy(src, p, c, chunk_sems.at[src, p, c], 0).wait_send()
+        part_copy(src, part_sems.at[src], 0).wait_send()
+
     def drain(src, carry):
-        @pl.when(jnp.logical_and(inner, src != z + 1))
-        def _():
-            for p in range(pairs):
-                for c in range(CUTS):
-                    chunk_copy(src, p, c, fwd_send.at[src, p, c], 0).wait_send()
-            part_copy(src, fwd_part_send.at[src], 0).wait_send()
+        sent = jnp.where(edge, src >= n - TAIL, jnp.logical_and(z < n - 1, src != z + 1))
+
+        @pl.when(sent)
+        def _():
+            left(src, fwd_send, fwd_part_send)
+
+        @pl.when(jnp.logical_and(hub, jnp.logical_and(src > 0, src < n - TAIL)))
+        def _():
+            left(src, zero_send, zero_part_send)
 
         return carry
 
@@ -261,7 +345,8 @@
             dma((n, pairs, CUTS)), dma((n,)),
             dma((pairs, CUTS)), dma,
             dma((n, pairs, CUTS)), dma((n,)),
-            pltpu.SemaphoreType.REGULAR,
+            dma((n, pairs, CUTS)), dma((n,)),
+            pltpu.SemaphoreType.REGULAR, pltpu.SemaphoreType.REGULAR,
         ],
         compiler_params=pltpu.CompilerParams(collective_id=0, has_side_effects=True),
     )(queries, page_table, page_table, lengths, keep_threshold.T, k_cache, v_cache)

time: 71.5 us -> 60 us (0.84)
  the two profiles are of different devices: /device:TPU:1728 before, /device:TPU:78 now
where the time goes in v3:
time: 60 us; the launch traced here: 59.9 us
  Pallas kernels  59.2 us (99%)
  between operations  0.64 us (1%)
    pallas_call x1, Pallas kernels, shards(): pl.pallas_call(attend, out_shape=tuple((pltpu.VMEM(*result) for result in...  58.6 us

profile of v3, /device:TPU:78, one launch (start us, length us, event | category | flops | bytes accessed | tf_op | source)
XLA Modules:
  0.0 59.9 jit_solution(12253256052218867985)
XLA Ops:
  0.6 58.6 %shard_map.85 = (bf16[4,512]{1,0:T(4,128)(2,1)S(1)}, f32[4,2,1024]{2,1,0:T(2,128)S(1)}, f32[4,2,8]{2,1,0:T(2,128)S(1)}) custom-call(bf16[4,512]{1,0:T(4,128)(2,1)} %q_ref.1, s32[4,128]{1,0:T(4,128)} %pt_ref.1, s32[4,128]{1,0:T(4,128)} %pt_ref.1, s32[4]{0:T(128)} %len_ref.1, s32[2,4]{1,0:T(2,128)} %bitcast.1, bf16[4,2,1024,128]{3,2,1,0:T(8,128)(2,1)} %k_hbm.1, ...), custom_call_target="tpu_custom_call" | custom-call | tf_op jit(solution)/shard_map/pallas_call | solution.py:333
  59.2 0.6 %shard_map.86 = (bf16[4,512]{1,0:T(4,128)(2,1)}, f32[4,2,1024]{2,1,0:T(2,128)}, f32[4,2,8]{2,1,0:T(2,128)}) custom-call(bf16[4,512]{1,0:T(4,128)(2,1)S(1)} %get-tuple-element.6.refs_0_, f32[4,2,1024]{2,1,0:T(2,128)S(1)} %get-tuple-element.7.refs_1_, f32[4,2,8]{2,1,0:T(2,128)S(1)} %get-tuple-element.8.refs_2_), custom_call_target="tpu_custom_call" | custom-call | tf_op jit(solution)/shard_map/pallas_call | solution.py:353

commit v4 on v2

v4 whole, which is shorter than its diff:
```python
import jax
import jax.numpy as jnp
from jax import lax
from jax.experimental import pallas as pl
from jax.experimental.pallas import tpu as pltpu
from jax.sharding import PartitionSpec as P

PAGE = 128
TAIL = 2
CUTS = 2
MESH = pl.DeviceIdType.MESH

softcap = 50.0
query_scale = 1.0 / 12.0
quanta = 65536.0


def attend(
    q_hbm, pt_hbm, len_hbm, thr_hbm, k_hbm, v_hbm,
    att_ref, mass_ref, keep_ref,
    q_ref, pt_vec, pt_ref, len_ref, thr_ref, kbuf, vbuf, gath, att32,
    in_sem, k_sem, v_sem, recv, own_send, far_send, fwd_send, zero_send,
    ready, zero_ready, far_ready,
):
    n = lax.axis_size("seq")
    z = lax.axis_index("seq")
    requests = k_hbm.shape[0]
    pairs = requests // 2
    slots = k_hbm.shape[2] // PAGE
    extra = pairs * slots
    tiles = extra + pairs + 1
    per = slots // CUTS
    pieces = [(c * per, per) for c in range(pairs * CUTS)] + [(extra, pairs + 1)]
    rest = len(pieces) - 1

    mid_at = n // 4
    half = n // 2
    edge = z == 0
    hub = z == 1
    mid = z == mid_at
    bend = z == half - 1
    low_end = jnp.logical_and(z > mid_at, z < half)
    tail = z >= n - TAIL
    follows = z > 1
    passes_on = jnp.logical_and(z > 0, z < n - 1)

    small = [
        pltpu.make_async_copy(src, dst, in_sem.at[i])
        for i, (src, dst) in enumerate(
            [(q_hbm, q_ref), (pt_hbm, pt_vec), (len_hbm, len_ref), (pt_hbm, pt_ref), (thr_hbm, thr_ref)]
        )
    ]
    copies = []
    for r in range(requests):
        if r == 1:
            for copy in small:
                copy.start()
        k_copy = pltpu.make_async_copy(k_hbm.at[r], kbuf.at[r], k_sem.at[r])
        k_copy.start()
        copies.append(k_copy)
    v_copies = []
    for r in range(requests):
        v_copy = pltpu.make_async_copy(v_hbm.at[r], vbuf.at[r], v_sem.at[r])
        v_copy.start()
        v_copies.append(v_copy)

    barrier = pltpu.get_barrier_semaphore()

    def greet(target):
        pl.semaphore_signal(barrier, inc=1, device_id={"seq": target}, device_id_type=MESH)

    @pl.when(hub)
    def _():
        greet(0)
        for other in range(2, n):
            greet(other)

    @pl.when(edge)
    def _():
        for other in range(n - TAIL, n):
            greet(other)

    @pl.when(passes_on)
    def _():
        greet(z + 1)

    @pl.when(mid)
    def _():
        greet(0)
        for other in range(mid_at + 1, half + 1):
            greet(other)

    @pl.when(z == half)
    def _():
        for other in range(half + 1, n):
            greet(other)

    @pl.when(edge)
    def _():
        pl.semaphore_wait(barrier, 2)
        for feeder in (1, mid_at):
            pl.semaphore_signal(
                zero_ready, inc=1, device_id={"seq": feeder}, device_id_type=MESH
            )

    sub = lax.broadcasted_iota(jnp.int32, (8, PAGE), 0)
    lane = lax.broadcasted_iota(jnp.int32, (8, PAGE), 1)
    first = lax.rem(sub, 4) < 2
    for copy in small:
        copy.wait()
    queries = q_ref[...].astype(jnp.float32)

    def rows_of(even, odd):
        return jnp.where(first, even, odd)

    def piece_copy(src, i, send_sem, target):
        block = gath.at[pl.ds(src * tiles + pieces[i][0], pieces[i][1])]
        return pltpu.make_async_remote_copy(
            src_ref=block, dst_ref=block, send_sem=send_sem, recv_sem=recv.at[src, i],
            device_id={"seq": target}, device_id_type=MESH,
        )

    direct = jnp.logical_not(hub)
    target = jnp.where(tail, 0, 1)

    def send_own(i):
        @pl.when(direct)
        def _():
            piece_copy(z, i, own_send, target).start()

    def greeted():
        @pl.when(follows)
        def _():
            more = z > mid_at
            pl.semaphore_wait(barrier, 2 + more.astype(jnp.int32) + tail.astype(jnp.int32))
            pl.semaphore_signal(ready, inc=1, device_id={"seq": z - 1}, device_id_type=MESH)

        @pl.when(z == half)
        def _():
            pl.semaphore_signal(
                far_ready, inc=1, device_id={"seq": mid_at}, device_id_type=MESH
            )

        @pl.when(z == n - TAIL)
        def _():
            pl.semaphore_signal(
                zero_ready, inc=1, device_id={"seq": z - 1}, device_id_type=MESH
            )

    weights = []
    denoms = []
    for p in range(pairs):
        table = rows_of(pt_vec[2 * p : 2 * p + 1, :], pt_vec[2 * p + 1 : 2 * p + 2, :])
        length = rows_of(len_ref[2 * p], len_ref[2 * p + 1])
        lives = []
        for s in range(slots):
            hit = jnp.where(table == z * slots + s, lane, 0).astype(jnp.float32)
            logical = jnp.sum(hit, axis=1, keepdims=True).astype(jnp.int32)
            lives.append(logical * PAGE + lane < length)
        logits = None
        for ri in range(2):
            r = 2 * p + ri
            lhs = []
            for kv in range(2):
                row = ri * 2 + kv
                block = jnp.where(
                    sub == row,
                    queries[r : r + 1, (2 * kv) * PAGE : (2 * kv + 1) * PAGE],
                    jnp.where(
                        sub == 4 + row,
                        queries[r : r + 1, (2 * kv + 1) * PAGE : (2 * kv + 2) * PAGE],
                        0.0,
                    ),
                )
                lhs.append(block)
            lhs = jnp.concatenate(lhs, axis=1).astype(jnp.bfloat16)
            copies[r].wait()
            keys = jnp.concatenate([kbuf[r, 0], kbuf[r, 1]], axis=1)
            term = lax.dot_general(
                lhs, keys, (((1,), (1,)), ((), ())), preferred_element_type=jnp.float32
            )
            logits = term if logits is None else logits + term
        total = None
        parts = []
        for s in range(slots):
            tile = logits[:, s * PAGE : (s + 1) * PAGE]
            capped = softcap * jnp.tanh(tile * query_scale / softcap)
            tile = jnp.where(lives[s], jnp.exp(capped - softcap), 0.0)
            gath[z * tiles + p * slots + s] = tile
            parts.append(tile)
            total = tile if total is None else total + tile
        weights.append(jnp.concatenate(parts, axis=1).astype(jnp.bfloat16))
        denoms.append(jnp.sum(total, axis=1, keepdims=True))
        if p == 0:
            greeted()
        for c in range(CUTS):
            send_own(p * CUTS + c)

    gath[z * tiles + extra + pairs] = jnp.where(lane == 0, denoms[0], denoms[1])
    for p in range(pairs):
        numer = jnp.zeros((8, PAGE), jnp.float32)
        for ri in range(2):
            r = 2 * p + ri
            v_copies[r].wait()
            values = jnp.concatenate([vbuf[r, 0], vbuf[r, 1]], axis=1)
            out = jnp.dot(weights[p], values, preferred_element_type=jnp.float32)
            for kv in range(2):
                mine = lax.rem(sub, 4) == ri * 2 + kv
                numer = jnp.where(mine, out[:, kv * PAGE : (kv + 1) * PAGE], numer)
        gath[z * tiles + extra + p] = numer
    send_own(rest)
    last = z == n - 1
    before_tail = z == n - TAIL - 1
    for when, other in ((last, 1), (low_end, mid_at), (z > half, half), (before_tail, 0)):

        @pl.when(when)
        def _():
            if other == 0:
                pl.semaphore_wait(zero_ready, 1)
            for i in range(len(pieces)):
                piece_copy(z, i, own_send, other).start()

    def each(src, *steps):
        for i in range(len(pieces)):
            for whether, what in steps:

                @pl.when(whether)
                def _():
                    what(i)

    def down(src, up):
        goes = jnp.logical_and(z < n - 1, src != z + 1)
        goes = jnp.logical_and(goes, jnp.logical_or(z != half - 1, jnp.logical_and(src > 0, src < half)))
        goes = jnp.logical_and(
            goes,
            jnp.logical_or(z != mid_at - 1, jnp.logical_or(src < mid_at, src >= half)),
        )
        each(
            src,
            (src != z, lambda i: piece_copy(src, i, fwd_send, 0).wait_recv()),
            (goes, lambda i: piece_copy(src, i, fwd_send, z + 1).start()),
            (up, lambda i: piece_copy(src, i, zero_send, 0).start()),
        )

    def stretch(start, stop, up):
        def one(src, carry):
            down(src, up)
            return carry

        lax.fori_loop(start, stop, one, 0)

    never = z < 0

    @pl.when(jnp.logical_not(edge))
    def _():
        @pl.when(passes_on)
        def _():
            pl.semaphore_wait(ready, 1)

        @pl.when(mid)
        def _():
            pl.semaphore_wait(zero_ready, 1)

        stretch(1, half, mid)

        @pl.when(hub)
        def _():
            pl.semaphore_wait(zero_ready, 1)

        stretch(half, n - TAIL - 1, hub)
        stretch(n - TAIL - 1, n - TAIL, never)

        @pl.when(z < half)
        def _():
            down(0, never)

        @pl.when(mid)
        def _():
            pl.semaphore_wait(far_ready, 1)
            for i in range(len(pieces)):
                piece_copy(0, i, far_send, half).start()

        stretch(n - TAIL, n, never)

        @pl.when(z >= half)
        def _():
            down(0, never)

    @pl.when(edge)
    def _():
        always = z >= 0

        def hand_on(src, carry):
            for i in range(len(pieces)):
                piece_copy(src, i, fwd_send, 0).wait_recv()
                piece_copy(src, i, fwd_send, 1).start()
            return carry

        def take(src, carry):
            each(src, (always, lambda i: piece_copy(src, i, fwd_send, 0).wait_recv()))
            return carry

        lax.fori_loop(n - TAIL, n - 1, hand_on, 0)
        take(n - 1, 0)
        lax.fori_loop(1, n - TAIL, take, 0)

    def over_all(tile):
        return sum(gath[src * tiles + tile] for src in range(n))

    den = over_all(extra + pairs)
    for p in range(pairs):
        inv = 1.0 / jnp.sum(jnp.where(lane == p, den, 0.0), axis=1, keepdims=True)
        numer = over_all(extra + p) * inv
        for ri in range(2):
            r = 2 * p + ri
            for kv in range(2):
                for g in range(2):
                    row = g * 4 + ri * 2 + kv
                    h = 2 * kv + g
                    att32[r : r + 1, h * PAGE : (h + 1) * PAGE] = numer[row : row + 1]
        keep = jnp.zeros((4, slots), jnp.float32)

        def page(r, j):
            slot = pt_ref[r, z * slots + j]
            owner = lax.div(slot, slots)
            return gath[owner * (tiles - slots) + slot + p * slots]

        for j in range(slots):
            tile = rows_of(page(2 * p, j), page(2 * p + 1, j)) * inv
            mass = tile[:4] + tile[4:]
            for ri in range(2):
                mass_ref[2 * p + ri, :, j * PAGE : (j + 1) * PAGE] = mass[2 * ri : 2 * ri + 2]
            column = lax.broadcasted_iota(jnp.int32, (4, slots), 1)
            keep = jnp.where(column == j, jnp.sum(mass, axis=1, keepdims=True), keep)
        for ri in range(2):
            r = 2 * p + ri
            which = lax.broadcasted_iota(jnp.int32, (2, slots), 0)
            thr = jnp.where(which == 0, thr_ref[0, r], thr_ref[1, r]).astype(jnp.float32)
            keep_ref[r] = jnp.minimum(1.0, quanta * keep[2 * ri : 2 * ri + 2] / thr)
    att_ref[...] = att32[...].astype(att_ref.dtype)

    def sent(amount, sem):
        region = gath.at[pl.ds(0, amount)]
        pltpu.make_async_remote_copy(
            src_ref=region, dst_ref=region, send_sem=sem, recv_sem=recv.at[0, 0],
            device_id={"seq": 0}, device_id_type=MESH,
        ).wait_send()

    thrice = jnp.logical_or(last, before_tail)
    twice = jnp.logical_and(jnp.logical_or(low_end, z > half), jnp.logical_not(thrice))
    once = jnp.logical_not(jnp.logical_or(twice, thrice))
    skips = z == mid_at - 1
    others = jnp.logical_not(jnp.logical_or(bend, skips))
    for when, amount, sem in (
        (jnp.logical_and(direct, once), tiles, own_send),
        (twice, 2 * tiles, own_send),
        (thrice, 3 * tiles, own_send),
        (mid, tiles, far_send),
        (edge, (TAIL - 1) * tiles, fwd_send),
        (jnp.logical_and(passes_on, others), (n - 1) * tiles, fwd_send),
        (skips, (n + mid_at - half) * tiles, fwd_send),
        (bend, (half - 1) * tiles, fwd_send),
        (mid, (half - 1) * tiles, zero_send),
        (hub, (n - TAIL - 1 - half) * tiles, zero_send),
    ):

        @pl.when(when)
        def _():
            sent(amount, sem)


def put_out(*refs):
    count = len(refs) // 2
    sems = refs[-1]
    ins, outs = refs[:count], refs[count : 2 * count]
    moves = [pltpu.make_async_copy(i, o, sems.at[k]) for k, (i, o) in enumerate(zip(ins, outs))]
    for move in moves:
        move.start()
    for move in moves:
        move.wait()


def shards(queries, k_cache, v_cache, page_table, lengths, keep_threshold):
    n = lax.axis_size("seq")
    requests, kv_local, tok_local, head_size = k_cache.shape
    slots = tok_local // PAGE
    vmem = pl.BlockSpec(memory_space=pltpu.VMEM)
    hbm = pl.BlockSpec(memory_space=pl.ANY)
    dma = pltpu.SemaphoreType.DMA
    pairs = requests // 2
    results = (
        (queries.shape, jnp.bfloat16),
        ((requests, kv_local, tok_local), jnp.float32),
        ((requests, kv_local, slots), jnp.float32),
    )
    tiles = pairs * slots + pairs + 1
    regular = pltpu.SemaphoreType.REGULAR
    held = pl.pallas_call(
        attend,
        out_shape=tuple(pltpu.VMEM(*result) for result in results),
        in_specs=[hbm] * 6,
        out_specs=(vmem, vmem, vmem),
        scratch_shapes=[
            pltpu.VMEM(queries.shape, queries.dtype),
            pltpu.VMEM(page_table.shape, jnp.int32),
            pltpu.SMEM(page_table.shape, jnp.int32),
            pltpu.SMEM(lengths.shape, jnp.int32),
            pltpu.SMEM(keep_threshold.shape[::-1], jnp.int32),
            pltpu.VMEM(k_cache.shape, k_cache.dtype),
            pltpu.VMEM(v_cache.shape, v_cache.dtype),
            pltpu.VMEM((n * tiles, 8, PAGE), jnp.float32),
            pltpu.VMEM(queries.shape, jnp.float32),
            dma((5,)), dma((requests,)), dma((requests,)),
            dma((n, pairs * CUTS + 1)), dma, dma, dma, dma,
            regular, regular, regular,
        ],
        compiler_params=pltpu.CompilerParams(collective_id=0, has_side_effects=True),
    )(queries, page_table, lengths, keep_threshold.T, k_cache, v_cache)
    return pl.pallas_call(
        put_out,
        out_shape=tuple(jax.ShapeDtypeStruct(*result) for result in results),
        in_specs=[vmem] * 3,
        out_specs=(hbm, hbm, hbm),
        scratch_shapes=[dma((3,))],
    )(*(pltpu.with_memory_space_constraint(h, pltpu.VMEM) for h in held))


def solution(mesh):
    placed = (
        P(("grp", "rep"), "head"),
        P(("grp", "rep"), "head", "seq", None),
        P(("grp", "rep"), "head", "seq", None),
        P(("grp", "rep"), None),
        P(("grp", "rep")),
        P(("grp", "rep"), "head"),
    )
    return jax.shard_map(
        shards,
        mesh=mesh,
        in_specs=placed,
        out_specs=(
            P(("grp", "rep"), "head"),
            P(("grp", "rep"), "head", "seq"),
            P(("grp", "rep"), "head", "seq"),
        ),
        check_vma=False,
    )
```

time: 71.5 us -> 54.7 us (0.77)
  the two profiles are of different devices: /device:TPU:1728 before, /device:TPU:1856 now
where the time goes in v4:
time: 54.7 us; the launch traced here: 54.5 us
  Pallas kernels  53.9 us (99%)
  between operations  0.64 us (1%)
    pallas_call x1, Pallas kernels, shards(): pl.pallas_call(attend, out_shape=tuple((pltpu.VMEM(*result) for result in...  53.2 us

profile of v4, /device:TPU:1856, one launch (start us, length us, event | category | flops | bytes accessed | tf_op | source)
XLA Modules:
  0.0 54.5 jit_solution(8680539788751886031)
XLA Ops:
  0.6 53.2 %shard_map.85 = (bf16[4,512]{1,0:T(4,128)(2,1)S(1)}, f32[4,2,1024]{2,1,0:T(2,128)S(1)}, f32[4,2,8]{2,1,0:T(2,128)S(1)}) custom-call(bf16[4,512]{1,0:T(4,128)(2,1)} %q_hbm.1, s32[4,128]{1,0:T(4,128)} %pt_hbm.1, s32[4]{0:T(128)} %len_hbm.1, s32[2,4]{1,0:T(2,128)} %bitcast.1, bf16[4,2,1024,128]{3,2,1,0:T(8,128)(2,1)} %k_hbm.1, bf16[4,2,1024,128]{3,2,1,0:T(8,128)(2,1)} %v_hbm.1), custom_call_target="tpu_custom_call" | custom-call | tf_op jit(solution)/shard_map/pallas_call | solution.py:398
  53.9 0.6 %shard_map.86 = (bf16[4,512]{1,0:T(4,128)(2,1)}, f32[4,2,1024]{2,1,0:T(2,128)}, f32[4,2,8]{2,1,0:T(2,128)}) custom-call(bf16[4,512]{1,0:T(4,128)(2,1)S(1)} %get-tuple-element.6.refs_0_, f32[4,2,1024]{2,1,0:T(2,128)S(1)} %get-tuple-element.7.refs_1_, f32[4,2,8]{2,1,0:T(2,128)S(1)} %get-tuple-element.8.refs_2_), custom_call_target="tpu_custom_call" | custom-call | tf_op jit(solution)/shard_map/pallas_call | solution.py:419

commit v5 on v4

--- a/solution.py
+++ b/solution.py
@@ -6,7 +6,7 @@
 from jax.sharding import PartitionSpec as P
 
 PAGE = 128
-TAIL = 2
+TAIL = 3
 CUTS = 2
 MESH = pl.DeviceIdType.MESH
 
@@ -19,7 +19,7 @@
     q_hbm, pt_hbm, len_hbm, thr_hbm, k_hbm, v_hbm,
     att_ref, mass_ref, keep_ref,
     q_ref, pt_vec, pt_ref, len_ref, thr_ref, kbuf, vbuf, gath, att32,
-    in_sem, k_sem, v_sem, recv, own_send, far_send, fwd_send, zero_send,
+    in_sem, k_sem, v_sem, recv, recv_low, own_send, end_send, far_send, fwd_send, zero_send,
     ready, zero_ready, far_ready,
 ):
     n = lax.axis_size("seq")
@@ -33,16 +33,31 @@
     pieces = [(c * per, per) for c in range(pairs * CUTS)] + [(extra, pairs + 1)]
     rest = len(pieces) - 1
 
-    mid_at = n // 4
     half = n // 2
+    jump_at = half - 2
+    column = lax.axis_index("grp") + lax.axis_index("head") + lax.axis_index("rep")
+    zero_first = column > 0
+    zero_late = column == 0
     edge = z == 0
     hub = z == 1
-    mid = z == mid_at
     bend = z == half - 1
-    low_end = jnp.logical_and(z > mid_at, z < half)
     tail = z >= n - TAIL
     follows = z > 1
     passes_on = jnp.logical_and(z > 0, z < n - 1)
+
+    barrier = pltpu.get_barrier_semaphore()
+
+    def greet(target):
+        pl.semaphore_signal(barrier, inc=1, device_id={"seq": target}, device_id_type=MESH)
+
+    @pl.when(edge)
+    def _():
+        greet(n - 1)
+
+        @pl.when(zero_first)
+        def _():
+            for other in range(n - TAIL, n - 1):
+                greet(other)
 
     small = [
         pltpu.make_async_copy(src, dst, in_sem.at[i])
@@ -52,22 +67,14 @@
     ]
     copies = []
     for r in range(requests):
-        if r == 1:
+        if r == 2:
             for copy in small:
                 copy.start()
         k_copy = pltpu.make_async_copy(k_hbm.at[r], kbuf.at[r], k_sem.at[r])
         k_copy.start()
         copies.append(k_copy)
-    v_copies = []
-    for r in range(requests):
-        v_copy = pltpu.make_async_copy(v_hbm.at[r], vbuf.at[r], v_sem.at[r])
-        v_copy.start()
-        v_copies.append(v_copy)
-
-    barrier = pltpu.get_barrier_semaphore()
-
-    def greet(target):
-        pl.semaphore_signal(barrier, inc=1, device_id={"seq": target}, device_id_type=MESH)
+    v_copy = pltpu.make_async_copy(v_hbm, vbuf, v_sem)
+    v_copy.start()
 
     @pl.when(hub)
     def _():
@@ -75,20 +82,13 @@
         for other in range(2, n):
             greet(other)
 
-    @pl.when(edge)
-    def _():
-        for other in range(n - TAIL, n):
-            greet(other)
-
     @pl.when(passes_on)
     def _():
         greet(z + 1)
 
-    @pl.when(mid)
-    def _():
-        greet(0)
-        for other in range(mid_at + 1, half + 1):
-            greet(other)
+    @pl.when(z == jump_at)
+    def _():
+        greet(half)
 
     @pl.when(z == half)
     def _():
@@ -97,11 +97,11 @@
 
     @pl.when(edge)
     def _():
-        pl.semaphore_wait(barrier, 2)
-        for feeder in (1, mid_at):
-            pl.semaphore_signal(
-                zero_ready, inc=1, device_id={"seq": feeder}, device_id_type=MESH
-            )
+        pl.semaphore_wait(barrier, 1)
+
+        @pl.when(zero_first)
+        def _():
+            pl.semaphore_signal(zero_ready, inc=1, device_id={"seq": 1}, device_id_type=MESH)
 
     sub = lax.broadcasted_iota(jnp.int32, (8, PAGE), 0)
     lane = lax.broadcasted_iota(jnp.int32, (8, PAGE), 1)
@@ -116,35 +116,47 @@
     def piece_copy(src, i, send_sem, target):
         block = gath.at[pl.ds(src * tiles + pieces[i][0], pieces[i][1])]
         return pltpu.make_async_remote_copy(
-            src_ref=block, dst_ref=block, send_sem=send_sem, recv_sem=recv.at[src, i],
+            src_ref=block, dst_ref=block, send_sem=send_sem,
+            recv_sem=recv.at[jnp.maximum(src - half + 1, 0), i],
             device_id={"seq": target}, device_id_type=MESH,
         )
 
+    coarse = [(0, tiles // 2), (tiles // 2, tiles - tiles // 2)]
+
+    def coarse_copy(src, i, send_sem, target):
+        block = gath.at[pl.ds(src * tiles + coarse[i][0], coarse[i][1])]
+        return pltpu.make_async_remote_copy(
+            src_ref=block, dst_ref=block, send_sem=send_sem, recv_sem=recv_low.at[src, i],
+            device_id={"seq": target}, device_id_type=MESH,
+        )
+
     direct = jnp.logical_not(hub)
-    target = jnp.where(tail, 0, 1)
+    low = jnp.logical_and(z > 1, z < half)
+    to_zero = jnp.logical_and(tail, zero_first)
+    target = jnp.where(to_zero, 0, 1)
+
+    last = z == n - 1
+    waits = jnp.logical_and(tail, jnp.logical_not(last))
+    goes_on = jnp.logical_or(edge, jnp.logical_and(z >= half, jnp.logical_not(waits)))
 
     def send_own(i):
-        @pl.when(direct)
+        @pl.when(goes_on)
         def _():
             piece_copy(z, i, own_send, target).start()
 
     def greeted():
         @pl.when(follows)
         def _():
-            more = z > mid_at
-            pl.semaphore_wait(barrier, 2 + more.astype(jnp.int32) + tail.astype(jnp.int32))
+            count = 2
+            for more in (z == half, z > half, jnp.logical_or(to_zero, z == n - 1)):
+                count = count + more.astype(jnp.int32)
+            pl.semaphore_wait(barrier, count)
             pl.semaphore_signal(ready, inc=1, device_id={"seq": z - 1}, device_id_type=MESH)
 
         @pl.when(z == half)
         def _():
             pl.semaphore_signal(
-                far_ready, inc=1, device_id={"seq": mid_at}, device_id_type=MESH
-            )
-
-        @pl.when(z == n - TAIL)
-        def _():
-            pl.semaphore_signal(
-                zero_ready, inc=1, device_id={"seq": z - 1}, device_id_type=MESH
+                far_ready, inc=1, device_id={"seq": jump_at}, device_id_type=MESH
             )
 
     weights = []
@@ -192,16 +204,20 @@
         weights.append(jnp.concatenate(parts, axis=1).astype(jnp.bfloat16))
         denoms.append(jnp.sum(total, axis=1, keepdims=True))
         if p == 0:
-            greeted()
+
+            @pl.when(jnp.logical_not(waits))
+            def _():
+                greeted()
+
         for c in range(CUTS):
             send_own(p * CUTS + c)
 
     gath[z * tiles + extra + pairs] = jnp.where(lane == 0, denoms[0], denoms[1])
+    v_copy.wait()
     for p in range(pairs):
         numer = jnp.zeros((8, PAGE), jnp.float32)
         for ri in range(2):
             r = 2 * p + ri
-            v_copies[r].wait()
             values = jnp.concatenate([vbuf[r, 0], vbuf[r, 1]], axis=1)
             out = jnp.dot(weights[p], values, preferred_element_type=jnp.float32)
             for kv in range(2):
@@ -209,42 +225,51 @@
                 numer = jnp.where(mine, out[:, kv * PAGE : (kv + 1) * PAGE], numer)
         gath[z * tiles + extra + p] = numer
     send_own(rest)
-    last = z == n - 1
-    before_tail = z == n - TAIL - 1
-    for when, other in ((last, 1), (low_end, mid_at), (z > half, half), (before_tail, 0)):
-
-        @pl.when(when)
-        def _():
-            if other == 0:
-                pl.semaphore_wait(zero_ready, 1)
-            for i in range(len(pieces)):
-                piece_copy(z, i, own_send, other).start()
-
-    def each(src, *steps):
+
+    @pl.when(waits)
+    def _():
+        greeted()
         for i in range(len(pieces)):
-            for whether, what in steps:
-
-                @pl.when(whether)
-                def _():
-                    what(i)
-
-    def down(src, up):
-        goes = jnp.logical_and(z < n - 1, src != z + 1)
-        goes = jnp.logical_and(goes, jnp.logical_or(z != half - 1, jnp.logical_and(src > 0, src < half)))
+            piece_copy(z, i, own_send, target).start()
+
+    @pl.when(jnp.logical_and(last, zero_first))
+    def _():
+        piece_copy(z, rest, end_send, 1).start()
+
+    @pl.when(low)
+    def _():
+        for i in range(len(coarse)):
+            coarse_copy(z, i, own_send, 1).start()
+
+    @pl.when(z > half)
+    def _():
+        for i in range(len(pieces)):
+            piece_copy(z, i, own_send, half).start()
+
+    def down(src, up, lower):
+        after = jnp.where(z < n - 1, z + 1, 0)
+        goes = jnp.logical_and(jnp.logical_or(z < n - 1, zero_late), src != after)
         goes = jnp.logical_and(
-            goes,
-            jnp.logical_or(z != mid_at - 1, jnp.logical_or(src < mid_at, src >= half)),
+            goes, jnp.logical_or(z != half - 1, jnp.logical_and(src > 0, src < half))
         )
-        each(
-            src,
-            (src != z, lambda i: piece_copy(src, i, fwd_send, 0).wait_recv()),
-            (goes, lambda i: piece_copy(src, i, fwd_send, z + 1).start()),
-            (up, lambda i: piece_copy(src, i, zero_send, 0).start()),
-        )
-
-    def stretch(start, stop, up):
+        copy = coarse_copy if lower else piece_copy
+        for i in range(len(coarse if lower else pieces)):
+
+            @pl.when(src != z)
+            def _():
+                copy(src, i, fwd_send, 0).wait_recv()
+
+            @pl.when(goes)
+            def _():
+                copy(src, i, fwd_send, after).start()
+
+            @pl.when(up)
+            def _():
+                copy(src, i, zero_send, 0).start()
+
+    def stretch(start, stop, up, lower=False):
         def one(src, carry):
-            down(src, up)
+            down(src, up, lower)
             return carry
 
         lax.fori_loop(start, stop, one, 0)
@@ -257,52 +282,77 @@
         def _():
             pl.semaphore_wait(ready, 1)
 
-        @pl.when(mid)
+        feeds = jnp.logical_and(hub, zero_first)
+
+        @pl.when(feeds)
         def _():
             pl.semaphore_wait(zero_ready, 1)
 
-        stretch(1, half, mid)
-
-        @pl.when(hub)
-        def _():
-            pl.semaphore_wait(zero_ready, 1)
-
-        stretch(half, n - TAIL - 1, hub)
-        stretch(n - TAIL - 1, n - TAIL, never)
-
         @pl.when(z < half)
         def _():
-            down(0, never)
-
-        @pl.when(mid)
-        def _():
-            pl.semaphore_wait(far_ready, 1)
-            for i in range(len(pieces)):
-                piece_copy(0, i, far_send, half).start()
+            stretch(1, half, feeds, True)
+
+        stretch(half, n - TAIL, feeds)
+
+        def block_zero():
+            down(0, never, False)
+
+            @pl.when(z == jump_at)
+            def _():
+                pl.semaphore_wait(far_ready, 1)
+                for i in range(len(pieces)):
+                    piece_copy(0, i, far_send, half).start()
+
+        @pl.when(jnp.logical_and(z < half, zero_first))
+        def _():
+            block_zero()
 
         stretch(n - TAIL, n, never)
 
+        @pl.when(jnp.logical_and(z < half, zero_late))
+        def _():
+            block_zero()
+
         @pl.when(z >= half)
         def _():
-            down(0, never)
+            stretch(1, half, never, True)
+            down(0, never, False)
 
     @pl.when(edge)
     def _():
-        always = z >= 0
-
         def hand_on(src, carry):
             for i in range(len(pieces)):
                 piece_copy(src, i, fwd_send, 0).wait_recv()
-                piece_copy(src, i, fwd_send, 1).start()
+                if i < rest:
+                    piece_copy(src, i, fwd_send, 1).start()
+                else:
+
+                    @pl.when(src < n - 1)
+                    def _():
+                        piece_copy(src, i, fwd_send, 1).start()
+
             return carry
 
         def take(src, carry):
-            each(src, (always, lambda i: piece_copy(src, i, fwd_send, 0).wait_recv()))
+            for i in range(len(pieces)):
+                piece_copy(src, i, fwd_send, 0).wait_recv()
             return carry
 
-        lax.fori_loop(n - TAIL, n - 1, hand_on, 0)
-        take(n - 1, 0)
-        lax.fori_loop(1, n - TAIL, take, 0)
+        def take_low(src, carry):
+            for i in range(len(coarse)):
+                coarse_copy(src, i, fwd_send, 0).wait_recv()
+            return carry
+
+        @pl.when(zero_first)
+        def _():
+            lax.fori_loop(n - TAIL, n, hand_on, 0)
+
+        @pl.when(zero_late)
+        def _():
+            lax.fori_loop(n - TAIL, n, take, 0)
+
+        lax.fori_loop(1, half, take_low, 0)
+        lax.fori_loop(half, n - TAIL, take, 0)
 
     def over_all(tile):
         return sum(gath[src * tiles + tile] for src in range(n))
@@ -346,22 +396,18 @@
             device_id={"seq": 0}, device_id_type=MESH,
         ).wait_send()
 
-    thrice = jnp.logical_or(last, before_tail)
-    twice = jnp.logical_and(jnp.logical_or(low_end, z > half), jnp.logical_not(thrice))
-    once = jnp.logical_not(jnp.logical_or(twice, thrice))
-    skips = z == mid_at - 1
-    others = jnp.logical_not(jnp.logical_or(bend, skips))
+    twice = z > half
+    once = jnp.logical_not(twice)
     for when, amount, sem in (
         (jnp.logical_and(direct, once), tiles, own_send),
         (twice, 2 * tiles, own_send),
-        (thrice, 3 * tiles, own_send),
-        (mid, tiles, far_send),
-        (edge, (TAIL - 1) * tiles, fwd_send),
-        (jnp.logical_and(passes_on, others), (n - 1) * tiles, fwd_send),
-        (skips, (n + mid_at - half) * tiles, fwd_send),
+        (jnp.logical_and(last, zero_first), pairs + 1, end_send),
+        (z == jump_at, tiles, far_send),
+        (jnp.logical_and(edge, zero_first), TAIL * tiles - pairs - 1, fwd_send),
+        (jnp.logical_and(passes_on, jnp.logical_not(bend)), (n - 1) * tiles, fwd_send),
         (bend, (half - 1) * tiles, fwd_send),
-        (mid, (half - 1) * tiles, zero_send),
-        (hub, (n - TAIL - 1 - half) * tiles, zero_send),
+        (jnp.logical_and(last, zero_late), (n - 1) * tiles, fwd_send),
+        (jnp.logical_and(hub, zero_first), (n - TAIL - 1) * tiles, zero_send),
     ):
 
         @pl.when(when)
@@ -410,8 +456,8 @@
             pltpu.VMEM(v_cache.shape, v_cache.dtype),
             pltpu.VMEM((n * tiles, 8, PAGE), jnp.float32),
             pltpu.VMEM(queries.shape, jnp.float32),
-            dma((5,)), dma((requests,)), dma((requests,)),
-            dma((n, pairs * CUTS + 1)), dma, dma, dma, dma,
+            dma((5,)), dma((requests,)), dma,
+            dma((n // 2 + 1, pairs * CUTS + 1)), dma((n // 2, 2)), dma, dma, dma, dma, dma,
             regular, regular, regular,
         ],
         compiler_params=pltpu.CompilerParams(collective_id=0, has_side_effects=True),

time: 54.7 us -> 51.9 us (0.949)
  the two profiles are of different devices: /device:TPU:1856 before, /device:TPU:78 now
where the time goes in v5:
time: 51.9 us; the launch traced here: 51.4 us
  Pallas kernels  50.7 us (98%)
  between operations  0.64 us (1%)
    pallas_call x1, Pallas kernels, shards(): pl.pallas_call(attend, out_shape=tuple((pltpu.VMEM(*result) for result in...  50.1 us

profile of v5, /device:TPU:78, one launch (start us, length us, event | category | flops | bytes accessed | tf_op | source)
XLA Modules:
  0.0 51.4 jit_solution(13601045823571021617)
XLA Ops:
  0.6 50.1 %shard_map.85 = (bf16[4,512]{1,0:T(4,128)(2,1)S(1)}, f32[4,2,1024]{2,1,0:T(2,128)S(1)}, f32[4,2,8]{2,1,0:T(2,128)S(1)}) custom-call(bf16[4,512]{1,0:T(4,128)(2,1)} %q_hbm.1, s32[4,128]{1,0:T(4,128)} %pt_hbm.1, s32[4]{0:T(128)} %len_hbm.1, s32[2,4]{1,0:T(2,128)} %bitcast.1, bf16[4,2,1024,128]{3,2,1,0:T(8,128)(2,1)} %k_hbm.1, bf16[4,2,1024,128]{3,2,1,0:T(8,128)(2,1)} %v_hbm.1), custom_call_target="tpu_custom_call" | custom-call | tf_op jit(solution)/shard_map/pallas_call | solution.py:444
  50.7 0.6 %shard_map.86 = (bf16[4,512]{1,0:T(4,128)(2,1)}, f32[4,2,1024]{2,1,0:T(2,128)}, f32[4,2,8]{2,1,0:T(2,128)}) custom-call(bf16[4,512]{1,0:T(4,128)(2,1)S(1)} %get-tuple-element.6.refs_0_, f32[4,2,1024]{2,1,0:T(2,128)S(1)} %get-tuple-element.7.refs_1_, f32[4,2,8]{2,1,0:T(2,128)S(1)} %get-tuple-element.8.refs_2_), custom_call_target="tpu_custom_call" | custom-call | tf_op jit(solution)/shard_map/pallas_call | solution.py:465

commit v6 on v5

--- a/solution.py
+++ b/solution.py
@@ -8,6 +8,7 @@
 PAGE = 128
 TAIL = 3
 CUTS = 2
+HANDED = 3
 MESH = pl.DeviceIdType.MESH
 
 softcap = 50.0
@@ -32,6 +33,7 @@
     per = slots // CUTS
     pieces = [(c * per, per) for c in range(pairs * CUTS)] + [(extra, pairs + 1)]
     rest = len(pieces) - 1
+    direct_end = tiles - HANDED * per
 
     half = n // 2
     jump_at = half - 2
@@ -66,13 +68,14 @@
         )
     ]
     copies = []
-    for r in range(requests):
-        if r == 2:
+    for p in range(pairs):
+        two = pl.ds(2 * p, 2)
+        k_copy = pltpu.make_async_copy(k_hbm.at[two], kbuf.at[two], k_sem.at[p])
+        k_copy.start()
+        copies.append(k_copy)
+        if p == 0:
             for copy in small:
                 copy.start()
-        k_copy = pltpu.make_async_copy(k_hbm.at[r], kbuf.at[r], k_sem.at[r])
-        k_copy.start()
-        copies.append(k_copy)
     v_copy = pltpu.make_async_copy(v_hbm, vbuf, v_sem)
     v_copy.start()
 
@@ -136,8 +139,7 @@
     target = jnp.where(to_zero, 0, 1)
 
     last = z == n - 1
-    waits = jnp.logical_and(tail, jnp.logical_not(last))
-    goes_on = jnp.logical_or(edge, jnp.logical_and(z >= half, jnp.logical_not(waits)))
+    goes_on = jnp.logical_or(edge, z >= half)
 
     def send_own(i):
         @pl.when(goes_on)
@@ -186,7 +188,8 @@
                 )
                 lhs.append(block)
             lhs = jnp.concatenate(lhs, axis=1).astype(jnp.bfloat16)
-            copies[r].wait()
+            if ri == 0:
+                copies[p].wait()
             keys = jnp.concatenate([kbuf[r, 0], kbuf[r, 1]], axis=1)
             term = lax.dot_general(
                 lhs, keys, (((1,), (1,)), ((), ())), preferred_element_type=jnp.float32
@@ -204,10 +207,7 @@
         weights.append(jnp.concatenate(parts, axis=1).astype(jnp.bfloat16))
         denoms.append(jnp.sum(total, axis=1, keepdims=True))
         if p == 0:
-
-            @pl.when(jnp.logical_not(waits))
-            def _():
-                greeted()
+            greeted()
 
         for c in range(CUTS):
             send_own(p * CUTS + c)
@@ -226,15 +226,10 @@
         gath[z * tiles + extra + p] = numer
     send_own(rest)
 
-    @pl.when(waits)
-    def _():
-        greeted()
-        for i in range(len(pieces)):
-            piece_copy(z, i, own_send, target).start()
-
     @pl.when(jnp.logical_and(last, zero_first))
     def _():
-        piece_copy(z, rest, end_send, 1).start()
+        for i in range(HANDED, len(pieces)):
+            piece_copy(z, i, end_send, 1).start()
 
     @pl.when(low)
     def _():
@@ -323,7 +318,7 @@
         def hand_on(src, carry):
             for i in range(len(pieces)):
                 piece_copy(src, i, fwd_send, 0).wait_recv()
-                if i < rest:
+                if i < HANDED:
                     piece_copy(src, i, fwd_send, 1).start()
                 else:
 
@@ -401,9 +396,9 @@
     for when, amount, sem in (
         (jnp.logical_and(direct, once), tiles, own_send),
         (twice, 2 * tiles, own_send),
-        (jnp.logical_and(last, zero_first), pairs + 1, end_send),
+        (jnp.logical_and(last, zero_first), direct_end, end_send),
         (z == jump_at, tiles, far_send),
-        (jnp.logical_and(edge, zero_first), TAIL * tiles - pairs - 1, fwd_send),
+        (jnp.logical_and(edge, zero_first), TAIL * tiles - direct_end, fwd_send),
         (jnp.logical_and(passes_on, jnp.logical_not(bend)), (n - 1) * tiles, fwd_send),
         (bend, (half - 1) * tiles, fwd_send),
         (jnp.logical_and(last, zero_late), (n - 1) * tiles, fwd_send),
@@ -456,7 +451,7 @@
             pltpu.VMEM(v_cache.shape, v_cache.dtype),
             pltpu.VMEM((n * tiles, 8, PAGE), jnp.float32),
             pltpu.VMEM(queries.shape, jnp.float32),
-            dma((5,)), dma((requests,)), dma,
+            dma((5,)), dma((pairs,)), dma,
             dma((n // 2 + 1, pairs * CUTS + 1)), dma((n // 2, 2)), dma, dma, dma, dma, dma,
             regular, regular, regular,
         ],

time: 51.9 us -> 51.9 us (level)
  no operation moved by 1% of the time
where the time goes in v6:
time: 51.9 us; the launch traced here: 51.2 us
  Pallas kernels  50.6 us (97%)
  between operations  0.64 us (1%)
    pallas_call x1, Pallas kernels, shards(): pl.pallas_call(attend, out_shape=tuple((pltpu.VMEM(*result) for result in...  49.9 us

profile of v6, /device:TPU:78, one launch (start us, length us, event | category | flops | bytes accessed | tf_op | source)
XLA Modules:
  0.0 51.2 jit_solution(5641185099532622679)
XLA Ops:
  0.6 49.9 %shard_map.85 = (bf16[4,512]{1,0:T(4,128)(2,1)S(1)}, f32[4,2,1024]{2,1,0:T(2,128)S(1)}, f32[4,2,8]{2,1,0:T(2,128)S(1)}) custom-call(bf16[4,512]{1,0:T(4,128)(2,1)} %q_hbm.1, s32[4,128]{1,0:T(4,128)} %pt_hbm.1, s32[4]{0:T(128)} %len_hbm.1, s32[2,4]{1,0:T(2,128)} %bitcast.1, bf16[4,2,1024,128]{3,2,1,0:T(8,128)(2,1)} %k_hbm.1, bf16[4,2,1024,128]{3,2,1,0:T(8,128)(2,1)} %v_hbm.1), custom_call_target="tpu_custom_call" | custom-call | tf_op jit(solution)/shard_map/pallas_call | solution.py:439
  50.5 0.6 %shard_map.86 = (bf16[4,512]{1,0:T(4,128)(2,1)}, f32[4,2,1024]{2,1,0:T(2,128)}, f32[4,2,8]{2,1,0:T(2,128)}) custom-call(bf16[4,512]{1,0:T(4,128)(2,1)S(1)} %get-tuple-element.6.refs_0_, f32[4,2,1024]{2,1,0:T(2,128)S(1)} %get-tuple-element.7.refs_1_, f32[4,2,8]{2,1,0:T(2,128)S(1)} %get-tuple-element.8.refs_2_), custom_call_target="tpu_custom_call" | custom-call | tf_op jit(solution)/shard_map/pallas_call | solution.py:460
